TPU v7x, 32 devices: a whole 2x2x4 slice. The times are simulated.
32 devices in a mesh: pipe: 2 (over x), dp: 4 (over z), tensor: 4 (over y, core).
Axes of the slice: x: 2, y: 2, z: 4, core: 2. Of those that a mesh axis runs over, the one named last changes fastest.
Arguments:
- acts_in: bfloat16 [2, 512, 4096], P(None, 'dp', 'tensor'), may hold values from -6 to 6
- weights: bfloat16 [2, 4096, 4096], P('pipe', None, 'tensor'), may hold values from -0.046875 to 0.046875
- cotangent: bfloat16 [2, 512, 4096], P(None, 'dp', 'tensor'), may hold values from -6 to 6
- hist_act: float32 [2, 16], P('pipe'), may hold values from 2 to 12
- hist_weight: float32 [2, 16], P('pipe'), may hold values from 0.01 to 0.1
- hist_grad: float32 [2, 16], P('pipe'), may hold values from 2 to 12
Outputs:
- section_acts: bfloat16 [2, 2, 512, 4096], P('pipe', None, 'dp', 'tensor')
- section_grads: bfloat16 [2, 2, 512, 4096], P('pipe', None, 'dp', 'tensor')
- weight_grad: bfloat16 [2, 4096, 4096], P('pipe', 'dp', 'tensor')
- new_hist_act: float32 [2, 16], P('pipe')
- new_hist_weight: float32 [2, 16], P('pipe')
- new_hist_grad: float32 [2, 16], P('pipe')
All inputs are finite; a program needn't handle non-finite values.
Results may differ from a plain program's by a relative error of at most 0.025.
Values may be sent and summed in bfloat16 or wider, within the bound.
A program may use at most 128 MiB of HBM per device.

v0:
```python
import jax
import jax.numpy as jnp
from jax import lax
from jax.sharding import PartitionSpec as P


def shifted(value, axis, steps):
    count = lax.axis_size(axis)
    initial, last = (max(0, -steps), min(count, count - steps))
    return lax.ppermute(value, axis, [(source, source + steps) for source in range(initial, last)])


def quantize(values, factor, limit_value):
    return jnp.clip(values.astype(jnp.float32) * factor, -limit_value, limit_value).astype(
        jnp.bfloat16
    )


def roll_history(history, newest):
    return jnp.concatenate([jnp.reshape(newest, (1, 1)), history[:, :-1]], axis=1)


def place_row(buffer, slot_index, is_live, new_row):
    old_row = lax.dynamic_index_in_dim(buffer, slot_index, 0, keepdims=False)
    return lax.dynamic_update_index_in_dim(
        buffer, jnp.where(is_live, new_row, old_row), slot_index, 0
    )


def shards(acts_in, weights, cotangent, hist_act, hist_weight, hist_grad):
    section_index = lax.axis_index("pipe")
    section_count = lax.axis_size("pipe")
    micro_count = acts_in.shape[0]
    row_count = acts_in.shape[1]
    own_width = acts_in.shape[2]
    weight = weights[0]
    full_width = weight.shape[0]
    tick_count = micro_count + section_count - 1
    act_factor = 448.0 / jnp.max(hist_act)
    weight_factor = 448.0 / jnp.max(hist_weight)
    grad_factor = 57344.0 / jnp.max(hist_grad)
    forward_factor = 1.0 / (act_factor * weight_factor)
    backward_factor = 1.0 / (grad_factor * weight_factor)
    update_factor = 1.0 / (act_factor * grad_factor)
    quant_weight = quantize(weight, weight_factor, 448.0)
    weight_peak = jnp.max(jnp.abs(weight.astype(jnp.float32)))

    def forward_tick(tick_index, loop_state):
        incoming, outputs, stash, act_peak = loop_state
        micro_index = tick_index - section_index
        is_live = (micro_index >= 0) & (micro_index < micro_count)
        slot_index = jnp.clip(micro_index, 0, micro_count - 1)
        first_input = lax.dynamic_index_in_dim(acts_in, slot_index, 0, keepdims=False)
        section_input = jnp.where(section_index == 0, first_input, incoming)
        quant_local = quantize(section_input, act_factor, 448.0)
        quant_full = lax.all_gather(quant_local, "tensor", axis=1, tiled=True)
        mixed_terms = lax.cond(
            is_live,
            lambda operand: jnp.dot(operand, quant_weight, preferred_element_type=jnp.float32)
            * forward_factor,
            lambda operand: jnp.zeros((row_count, own_width), jnp.float32),
            quant_full,
        )
        section_output = (section_input.astype(jnp.float32) + mixed_terms).astype(jnp.bfloat16)
        outputs = place_row(outputs, slot_index, is_live, section_output)
        stash = place_row(stash, slot_index, is_live, quant_full)
        tick_peak = jnp.where(
            is_live, jnp.max(jnp.abs(section_input.astype(jnp.float32))), jnp.float32(0.0)
        )
        act_peak = jnp.maximum(act_peak, tick_peak)
        incoming = shifted(section_output, "pipe", 1)
        return (incoming, outputs, stash, act_peak)

    forward_init = (
        jnp.zeros((row_count, own_width), jnp.bfloat16),
        jnp.zeros((micro_count, row_count, own_width), jnp.bfloat16),
        jnp.zeros((micro_count, row_count, full_width), jnp.bfloat16),
        jnp.float32(0.0),
    )
    unused, outputs, stash, act_peak = lax.fori_loop(0, tick_count, forward_tick, forward_init)

    def backward_tick(tick_index, loop_state):
        incoming, grads_out, held, grad_peak = loop_state
        micro_index = tick_index - (section_count - 1 - section_index)
        is_live = (micro_index >= 0) & (micro_index < micro_count)
        slot_index = jnp.clip(micro_index, 0, micro_count - 1)
        last_weights = lax.dynamic_index_in_dim(cotangent, slot_index, 0, keepdims=False)
        last_output = lax.dynamic_index_in_dim(outputs, slot_index, 0, keepdims=False)
        last_input = (last_weights.astype(jnp.float32) * last_output.astype(jnp.float32)).astype(
            jnp.bfloat16
        )
        grad_input = jnp.where(section_index == section_count - 1, last_input, incoming)
        quant_grad = quantize(grad_input, grad_factor, 57344.0)
        partial_terms = lax.cond(
            is_live,
            lambda operand: lax.dot_general(
                operand, quant_weight, (((1,), (1,)), ((), ())), preferred_element_type=jnp.float32
            )
            * backward_factor,
            lambda operand: jnp.zeros((row_count, full_width), jnp.float32),
            quant_grad,
        )
        back_terms = lax.psum_scatter(
            partial_terms.astype(jnp.bfloat16), "tensor", scatter_dimension=1, tiled=True
        ).astype(jnp.float32)
        grad_output = (grad_input.astype(jnp.float32) + back_terms).astype(jnp.bfloat16)
        grads_out = place_row(grads_out, slot_index, is_live, grad_output)
        saved_acts = lax.dynamic_index_in_dim(stash, slot_index, 0, keepdims=False)
        held = lax.cond(
            is_live,
            lambda running: running
            + lax.dot_general(
                saved_acts, quant_grad, (((0,), (0,)), ((), ())), preferred_element_type=jnp.float32
            )
            * update_factor,
            lambda running: running,
            held,
        )
        tick_peak = jnp.where(
            is_live, jnp.max(jnp.abs(grad_input.astype(jnp.float32))), jnp.float32(0.0)
        )
        grad_peak = jnp.maximum(grad_peak, tick_peak)
        incoming = shifted(grad_output, "pipe", -1)
        return (incoming, grads_out, held, grad_peak)

    held_init = jnp.zeros((full_width, own_width), jnp.float32)
    backward_init = (
        jnp.zeros((row_count, own_width), jnp.bfloat16),
        jnp.zeros((micro_count, row_count, own_width), jnp.bfloat16),
        held_init,
        jnp.float32(0.0),
    )
    unused, grads_out, held, grad_peak = lax.fori_loop(0, tick_count, backward_tick, backward_init)
    weight_sums = lax.psum_scatter(held.astype(jnp.bfloat16), "dp", scatter_dimension=0, tiled=True)
    act_peak, weight_peak, grad_peak = lax.pmax(
        (act_peak, weight_peak, grad_peak), ("dp", "tensor")
    )
    return (
        outputs[None],
        grads_out[None],
        weight_sums[None],
        roll_history(hist_act, act_peak),
        roll_history(hist_weight, weight_peak),
        roll_history(hist_grad, grad_peak),
    )


def solution(mesh):
    placed = (
        P(None, "dp", "tensor"),
        P("pipe", None, "tensor"),
        P(None, "dp", "tensor"),
        P("pipe", None),
        P("pipe", None),
        P("pipe", None),
    )
    return jax.shard_map(
        shards,
        mesh=mesh,
        in_specs=placed,
        out_specs=(
            P("pipe", None, "dp", "tensor"),
            P("pipe", None, "dp", "tensor"),
            P("pipe", "dp", "tensor"),
            P("pipe", None),
            P("pipe", None),
            P("pipe", None),
        ),
        check_vma=False,
    )
```

profile of v0, /device:TPU:0, one launch (start us, length us, event | category | flops | bytes accessed | tf_op | source)
XLA Modules:
  0.0 469.6 jit_solution(13355030201614715578)
XLA Ops:
  8.0 1.3 reduce_max.67
  9.3 1.3 reduce_max.66
  10.5 1.3 reduce_max.65
  14.0 10.5 %fusion.15 = (f32[]{:T(128)}, bf16[4096,1024]{1,0:T(8,128)(2,1)}) fusion(bf16[1,4096,1024]{2,1,0:T(8,128)(2,1)} %param.17, f32[]{:T(128)S(6)} %div.19), kind=kLoop, calls=%fused_computation.37 | loop fusion | flops 25165824 | bytes 16777224 | tf_op jit(solution)/shard_map/reduce_max | solution.py:46
  25.2 0.9 broadcast.19.clone
  26.3 113.2 %while.44 = (s32[]{:T(128)}, bf16[128,1024]{1,0:T(8,128)(2,1)}, bf16[2,128,1024]{2,1,0:T(8,128)(2,1)}, bf16[2,128,4096]{2,1,0:T(8,128)(2,1)S(1)}, f32[]{:T(128)}...) while((s32[]{:T(128)}, bf16[128,1024]{1,0:T(8,128)(2,1)}, ...), condition=%wide.region_6.7_spmd, body=%wide.region_2.6_spmd.sunk | while | flops 1075970048 | bytes 23593332 | solution.py:80
  26.4 1.6 fusion.29
  29.5 1.7 constant_dynamic-slice_fusion.6
  31.2 17.5 %all-gather.2.cloned.1.call-done = bf16[128,4096]{1,0:T(8,128)(2,1)} async-done(((bf16[128,1024]{1,0:T(8,128)(2,1)}), bf16[128,4096]{1,0:T(8,128)(2,1)}) %all-gather.2.cloned.1.call-update) | async-done | bytes 1048592 | tf_op jit(solution)/shard_map/while/body/eval_jaxpr/all_gather | solution.py:56
  48.7 5.8 %conditional.6 = (f32[128,1024]{1,0:T(8,128)}) conditional(s32[]{:T(128)} %convert_element_type.215, () %tuple.108, (bf16[128,4096]{1,0:T(8,128)(2,1)}, bf16[4096,1024]{1,0:T(8,128)(2,1)}, f32[]{:T(128)}) %tuple.109), branch_computations={%region_3.3_spmd, %region_4.4_spmd} | conditional | flops 1073872896 | bytes 9961484 | solution.py:57
  48.7 5.8 %convolution_multiply_fusion = f32[128,1024]{1,0:T(8,128)} fusion(bf16[128,4096]{1,0:T(8,128)(2,1)} %get-tuple-element.548, bf16[4096,1024]{1,0:T(8,128)(2,1)} %get-tuple-element.549, f32[]{:T(128)} %get-tuple-element.550), kind=kOutput, calls=%fused_computation | convolution fusion | flops 1073872896 | bytes 9961476 | tf_op jit(solution)/shard_map/while/body/eval_jaxpr/cond/branch_1_fun/dot_general | solution.py:59
  54.5 1.9 bitcast_dynamic-update-slice_fusion.6
  56.4 2.0 collective-permute-start
  58.4 1.5 bitcast_dynamic-update-slice_fusion.7
  59.9 4.0 collective-permute-done
  63.9 1.6 fusion.29
  67.0 1.7 constant_dynamic-slice_fusion.6
  68.8 16.0 %all-gather.2.cloned.1.call-done = bf16[128,4096]{1,0:T(8,128)(2,1)} async-done(((bf16[128,1024]{1,0:T(8,128)(2,1)}), bf16[128,4096]{1,0:T(8,128)(2,1)}) %all-gather.2.cloned.1.call-update) | async-done | bytes 1048592 | tf_op jit(solution)/shard_map/while/body/eval_jaxpr/all_gather | solution.py:56
  84.7 5.8 %conditional.6 = (f32[128,1024]{1,0:T(8,128)}) conditional(s32[]{:T(128)} %convert_element_type.215, () %tuple.108, (bf16[128,4096]{1,0:T(8,128)(2,1)}, bf16[4096,1024]{1,0:T(8,128)(2,1)}, f32[]{:T(128)}) %tuple.109), branch_computations={%region_3.3_spmd, %region_4.4_spmd} | conditional | flops 1073872896 | bytes 9961484 | solution.py:57
  84.7 5.8 %convolution_multiply_fusion = f32[128,1024]{1,0:T(8,128)} fusion(bf16[128,4096]{1,0:T(8,128)(2,1)} %get-tuple-element.548, bf16[4096,1024]{1,0:T(8,128)(2,1)} %get-tuple-element.549, f32[]{:T(128)} %get-tuple-element.550), kind=kOutput, calls=%fused_computation | convolution fusion | flops 1073872896 | bytes 9961476 | tf_op jit(solution)/shard_map/while/body/eval_jaxpr/cond/branch_1_fun/dot_general | solution.py:59
  90.5 1.9 bitcast_dynamic-update-slice_fusion.6
  92.4 4.1 collective-permute-start
  96.5 1.5 bitcast_dynamic-update-slice_fusion.7
  98.0 3.7 collective-permute-done
  101.7 1.6 fusion.29
  104.8 1.7 constant_dynamic-slice_fusion.6
  106.6 15.9 %all-gather.2.cloned.1.call-done = bf16[128,4096]{1,0:T(8,128)(2,1)} async-done(((bf16[128,1024]{1,0:T(8,128)(2,1)}), bf16[128,4096]{1,0:T(8,128)(2,1)}) %all-gather.2.cloned.1.call-update) | async-done | bytes 1048592 | tf_op jit(solution)/shard_map/while/body/eval_jaxpr/all_gather | solution.py:56
  123.4 1.9 bitcast_dynamic-update-slice_fusion.6
  125.3 9.0 %collective-permute-start = (bf16[128,1024]{1,0:T(8,128)(2,1)S(1)}, bf16[128,1024]{1,0:T(8,128)(2,1)}, u32[]{:S(2)}, u32[]{:S(2)}) collective-permute-start(bf16[128,1024]{1,0:T(8,128)(2,1)S(1)} %get-tuple-element.816), channel_id=1, source_target_pairs={{0,16},{1,17},{2,18},{3,19},{4,20},{5,21},{6,22},{7,23},{8,24},{9,... | collective-permute-start | bytes 786440 | tf_op jit(solution)/shard_map/while/body/eval_jaxpr/ppermute | solution.py:10
  134.6 4.9 %collective-permute-done = bf16[128,1024]{1,0:T(8,128)(2,1)} collective-permute-done((bf16[128,1024]{1,0:T(8,128)(2,1)S(1)}, bf16[128,1024]{1,0:T(8,128)(2,1)}, u32[]{:S(2)}, u32[]{:S(2)}) %collective-permute-start) | collective-permute-done | bytes 262176 | tf_op jit(solution)/shard_map/while/body/eval_jaxpr/ppermute | solution.py:10
  141.1 7.9 %broadcast_in_dim.44 = f32[4096,1024]{1,0:T(8,128)} broadcast(f32[]{:T(128)} %constant.174.clone.1), dimensions={} | broadcast | bytes 16777220 | tf_op jit(solution)/shard_map/broadcast_in_dim | solution.py:126
  149.0 159.9 %while.45 = (s32[]{:T(128)}, bf16[128,1024]{1,0:T(8,128)(2,1)}, bf16[2,128,1024]{2,1,0:T(8,128)(2,1)}, f32[4096,1024]{1,0:T(8,128)}, f32[]{:T(128)}, /*index=5*/...) while((s32[]{:T(128)}, bf16[128,1024]{1,0:T(8,128)(2,1)}, ...), condition=%wide.region_15.16_spmd, body=%wide.region_8.15_spmd.sunk | while | flops 2159149056 | bytes 58196976 | solution.py:133
  149.0 1.9 fusion.31
  151.7 1.0 copy-done
  152.7 1.0 constant_dynamic-slice_fusion.8
  153.7 31.2 %reduce-scatter.5.cloned.1.call-done = bf16[128,1024]{1,0:T(8,128)(2,1)} async-done(((bf16[128,4096]{1,0:T(8,128)(2,1)}), bf16[128,1024]{1,0:T(8,128)(2,1)}) %reduce-scatter.5.cloned.1.call-update) | async-done | bytes 262160 | tf_op jit(solution)/shard_map/while/body/eval_jaxpr/reduce_scatter | solution.py:103
  184.9 1.9 bitcast_dynamic-update-slice_fusion.8
  186.8 1.3 collective-permute-start.1
  188.8 7.9 %collective-permute-done.1 = bf16[128,1024]{1,0:T(8,128)(2,1)} collective-permute-done((bf16[128,1024]{1,0:T(8,128)(2,1)S(1)}, bf16[128,1024]{1,0:T(8,128)(2,1)}, u32[]{:S(2)}, u32[]{:S(2)}) %collective-permute-start.1) | collective-permute-done | bytes 262176 | tf_op jit(solution)/shard_map/while/body/eval_jaxpr/ppermute | solution.py:10
  196.6 1.9 fusion.31
  199.2 6.3 %conditional.7 = (bf16[128,4096]{1,0:T(8,128)(2,1)S(1)}) conditional(s32[]{:T(128)} %convert_element_type.219, () %tuple.113, (bf16[128,1024]{1,0:T(8,128)(2,1)S(1)}, bf16[4096,1024]{1,0:T(8,128)(2,1)}, f32[]{:T(128)}) %tuple.114), branch_computations={%region_9.9_spmd, %region_10.10_spmd} | conditional | flops 1074790400 | bytes 9699340 | solution.py:94
  199.2 6.3 %convolution_multiply_fusion.1 = bf16[128,4096]{1,0:T(8,128)(2,1)S(1)} fusion(bf16[128,1024]{1,0:T(8,128)(2,1)S(1)} %get-tuple-element.563, bf16[4096,1024]{1,0:T(8,128)(2,1)} %get-tuple-element.564, f32[]{:T(128)} %get-tuple-element.565), kind=kOutput, calls=%fused_computation.15 | convolution fusion | flops 1074790400 | bytes 9699332 | tf_op jit(solution)/shard_map/while/body/eval_jaxpr/cond/branch_1_fun/dot_general | solution.py:96
  205.5 1.0 copy-done
  206.5 1.0 constant_dynamic-slice_fusion.8
  207.5 31.9 %reduce-scatter.5.cloned.1.call-done = bf16[128,1024]{1,0:T(8,128)(2,1)} async-done(((bf16[128,4096]{1,0:T(8,128)(2,1)}), bf16[128,1024]{1,0:T(8,128)(2,1)}) %reduce-scatter.5.cloned.1.call-update) | async-done | bytes 262160 | tf_op jit(solution)/shard_map/while/body/eval_jaxpr/reduce_scatter | solution.py:103
  239.4 1.9 bitcast_dynamic-update-slice_fusion.8
  241.2 1.3 collective-permute-start.1
  242.5 13.9 %conditional.8 = (f32[4096,1024]{1,0:T(8,128)}) conditional(s32[]{:T(128)} %convert_element_type.219, f32[4096,1024]{1,0:T(8,128)} %get-tuple-element.903, (bf16[2,128,4096]{2,1,0:T(8,128)(2,1)S(1)}, s32[]{:T(128)}, bf16[128,1024]{1,0:T(8,128)(2,1)S(1)}, f32[]{:T(128)}, f32[4096,1024]{1,0:T(8,128)}) %tuple.115), branch_computations={%region_12.12_spmd, %region_13.13_spmd} | conditional | flops 1082130432 | bytes 34865168 | solution.py:109
  242.5 13.9 %multiply_add_fusion = f32[4096,1024]{1,0:T(8,128)} fusion(f32[4096,1024]{1,0:T(8,128)} %get-tuple-element.566, bf16[128,1024]{1,0:T(8,128)(2,1)S(1)} %get-tuple-element.569, f32[]{:T(128)} %get-tuple-element.570, bf16[2,128,4096]{2,1,0:T(8,128)(2,1)S(1)} %get-tuple-element.567, s32[]{:T(128)} %get-tuple-element.568), kind=kOutput, calls=%fused_computation.16 | convolution fusion | flops 1082130432 | bytes 34865160 | tf_op jit(solution)/shard_map/while/body/eval_jaxpr/cond/branch_1_fun/dot_general | solution.py:112
  257.2 1.9 fusion.31
  259.8 6.3 %conditional.7 = (bf16[128,4096]{1,0:T(8,128)(2,1)S(1)}) conditional(s32[]{:T(128)} %convert_element_type.219, () %tuple.113, (bf16[128,1024]{1,0:T(8,128)(2,1)S(1)}, bf16[4096,1024]{1,0:T(8,128)(2,1)}, f32[]{:T(128)}) %tuple.114), branch_computations={%region_9.9_spmd, %region_10.10_spmd} | conditional | flops 1074790400 | bytes 9699340 | solution.py:94
  259.8 6.3 %convolution_multiply_fusion.1 = bf16[128,4096]{1,0:T(8,128)(2,1)S(1)} fusion(bf16[128,1024]{1,0:T(8,128)(2,1)S(1)} %get-tuple-element.563, bf16[4096,1024]{1,0:T(8,128)(2,1)} %get-tuple-element.564, f32[]{:T(128)} %get-tuple-element.565), kind=kOutput, calls=%fused_computation.15 | convolution fusion | flops 1074790400 | bytes 9699332 | tf_op jit(solution)/shard_map/while/body/eval_jaxpr/cond/branch_1_fun/dot_general | solution.py:96
  266.1 1.0 copy-done
  267.1 1.0 constant_dynamic-slice_fusion.8
  268.1 23.1 %reduce-scatter.5.cloned.1.call-done = bf16[128,1024]{1,0:T(8,128)(2,1)} async-done(((bf16[128,4096]{1,0:T(8,128)(2,1)}), bf16[128,1024]{1,0:T(8,128)(2,1)}) %reduce-scatter.5.cloned.1.call-update) | async-done | bytes 262160 | tf_op jit(solution)/shard_map/while/body/eval_jaxpr/reduce_scatter | solution.py:103
  291.1 1.9 bitcast_dynamic-update-slice_fusion.8
  293.0 1.3 collective-permute-start.1
  294.3 13.9 %conditional.8 = (f32[4096,1024]{1,0:T(8,128)}) conditional(s32[]{:T(128)} %convert_element_type.219, f32[4096,1024]{1,0:T(8,128)} %get-tuple-element.903, (bf16[2,128,4096]{2,1,0:T(8,128)(2,1)S(1)}, s32[]{:T(128)}, bf16[128,1024]{1,0:T(8,128)(2,1)S(1)}, f32[]{:T(128)}, f32[4096,1024]{1,0:T(8,128)}) %tuple.115), branch_computations={%region_12.12_spmd, %region_13.13_spmd} | conditional | flops 1082130432 | bytes 34865168 | solution.py:109
  294.3 13.9 %multiply_add_fusion = f32[4096,1024]{1,0:T(8,128)} fusion(f32[4096,1024]{1,0:T(8,128)} %get-tuple-element.566, bf16[128,1024]{1,0:T(8,128)(2,1)S(1)} %get-tuple-element.569, f32[]{:T(128)} %get-tuple-element.570, bf16[2,128,4096]{2,1,0:T(8,128)(2,1)S(1)} %get-tuple-element.567, s32[]{:T(128)} %get-tuple-element.568), kind=kOutput, calls=%fused_computation.16 | convolution fusion | flops 1082130432 | bytes 34865160 | tf_op jit(solution)/shard_map/while/body/eval_jaxpr/cond/branch_1_fun/dot_general | solution.py:112
  309.0 9.1 %convert_element_type.140 = bf16[4096,1024]{1,0:T(8,128)(2,1)} convert(f32[4096,1024]{1,0:T(8,128)} %get-tuple-element.601) | non-fusion elementwise | flops 4194304 | bytes 25165824 | tf_op jit(solution)/shard_map/convert_element_type | solution.py:134
  318.1 35.8 %all-reduce = (f32[1,1]{1,0:T(1,128)}, f32[1,1]{1,0:T(1,128)}, f32[1,1]{1,0:T(1,128)}) all-reduce(f32[1,1]{1,0:T(1,128)} %bitcast.13, f32[1,1]{1,0:T(1,128)} %bitcast.14, f32[1,1]{1,0:T(1,128)} %bitcast.15), channel_id=1, replica_groups=mesh['pipe'=2,'dp'=4,'tensor'=4] {'dp','tensor'}, use_global_device_ids=true, to_apply=%region_17.18 | all-reduce | flops 3 | bytes 24 | tf_op jit(solution)/shard_map/pmax | solution.py:135
  353.9 1.2 pad_maximum_fusion.2
  355.2 1.8 pad_maximum_fusion
  356.9 105.2 %reduce-scatter.3.cloned.1.call-done = bf16[1024,1024]{1,0:T(8,128)(2,1)} async-done(((bf16[4096,1024]{1,0:T(8,128)(2,1)}), bf16[1024,1024]{1,0:T(8,128)(2,1)}) %reduce-scatter.3.cloned.1.call-update) | async-done | bytes 2097168 | tf_op jit(solution)/shard_map/reduce_scatter | solution.py:134
  (50 shorter events, 9.7 us)
Async XLA Ops:
  26.3 22.4 %all-gather.2.cloned.1.call-start = ((), (), s32[]{:S(2)}) async-start(), calls=%async_computation.3 | async-start | bytes 1310720 | tf_op jit(solution)/shard_map/while/body/eval_jaxpr/all_gather | solution.py:56
  56.4 7.5 %collective-permute-start = (bf16[128,1024]{1,0:T(8,128)(2,1)S(1)}, bf16[128,1024]{1,0:T(8,128)(2,1)}, u32[]{:S(2)}, u32[]{:S(2)}) collective-permute-start(bf16[128,1024]{1,0:T(8,128)(2,1)S(1)} %get-tuple-element.816), channel_id=1, source_target_pairs={{0,16},{1,17},{2,18},{3,19},{4,20},{5,21},{6,22},{7,23},{8,24},{9,... | collective-permute-start | bytes 786440 | tf_op jit(solution)/shard_map/while/body/eval_jaxpr/ppermute | solution.py:10
  63.9 20.8 %all-gather.2.cloned.1.call-start = ((), (), s32[]{:S(2)}) async-start(), calls=%async_computation.3 | async-start | bytes 1310720 | tf_op jit(solution)/shard_map/while/body/eval_jaxpr/all_gather | solution.py:56
  92.4 9.3 %collective-permute-start = (bf16[128,1024]{1,0:T(8,128)(2,1)S(1)}, bf16[128,1024]{1,0:T(8,128)(2,1)}, u32[]{:S(2)}, u32[]{:S(2)}) collective-permute-start(bf16[128,1024]{1,0:T(8,128)(2,1)S(1)} %get-tuple-element.816), channel_id=1, source_target_pairs={{0,16},{1,17},{2,18},{3,19},{4,20},{5,21},{6,22},{7,23},{8,24},{9,... | collective-permute-start | bytes 786440 | tf_op jit(solution)/shard_map/while/body/eval_jaxpr/ppermute | solution.py:10
  101.7 20.8 %all-gather.2.cloned.1.call-start = ((), (), s32[]{:S(2)}) async-start(), calls=%async_computation.3 | async-start | bytes 1310720 | tf_op jit(solution)/shard_map/while/body/eval_jaxpr/all_gather | solution.py:56
  125.3 14.2 %collective-permute-start = (bf16[128,1024]{1,0:T(8,128)(2,1)S(1)}, bf16[128,1024]{1,0:T(8,128)(2,1)}, u32[]{:S(2)}, u32[]{:S(2)}) collective-permute-start(bf16[128,1024]{1,0:T(8,128)(2,1)S(1)} %get-tuple-element.816), channel_id=1, source_target_pairs={{0,16},{1,17},{2,18},{3,19},{4,20},{5,21},{6,22},{7,23},{8,24},{9,... | collective-permute-start | bytes 786440 | tf_op jit(solution)/shard_map/while/body/eval_jaxpr/ppermute | solution.py:10
  149.0 35.9 %reduce-scatter.5.cloned.1.call-start = ((), (), s32[]{:S(2)}) async-start(), calls=%async_computation.4 | async-start | bytes 1310720 | tf_op jit(solution)/shard_map/while/body/eval_jaxpr/reduce_scatter | solution.py:103
  150.9 0.7 copy-start.1
  151.7 1.0 copy-start
  186.8 9.9 %collective-permute-start.1 = (bf16[128,1024]{1,0:T(8,128)(2,1)S(1)}, bf16[128,1024]{1,0:T(8,128)(2,1)}, u32[]{:S(2)}, u32[]{:S(2)}) collective-permute-start(bf16[128,1024]{1,0:T(8,128)(2,1)S(1)} %get-tuple-element.834), channel_id=1, source_target_pairs={{16,0},{17,1},{18,2},{19,3},{20,4},{21,5},{22,6},{23,7},{24,8},{25... | collective-permute-start | bytes 786440 | tf_op jit(solution)/shard_map/while/body/eval_jaxpr/ppermute | solution.py:10
  196.6 42.7 %reduce-scatter.5.cloned.1.call-start = ((), (), s32[]{:S(2)}) async-start(), calls=%async_computation.4 | async-start | bytes 1310720 | tf_op jit(solution)/shard_map/while/body/eval_jaxpr/reduce_scatter | solution.py:103
  198.5 0.7 copy-start.1
  205.5 1.0 copy-start
  241.2 15.9 %collective-permute-start.1 = (bf16[128,1024]{1,0:T(8,128)(2,1)S(1)}, bf16[128,1024]{1,0:T(8,128)(2,1)}, u32[]{:S(2)}, u32[]{:S(2)}) collective-permute-start(bf16[128,1024]{1,0:T(8,128)(2,1)S(1)} %get-tuple-element.834), channel_id=1, source_target_pairs={{16,0},{17,1},{18,2},{19,3},{20,4},{21,5},{22,6},{23,7},{24,8},{25... | collective-permute-start | bytes 786440 | tf_op jit(solution)/shard_map/while/body/eval_jaxpr/ppermute | solution.py:10
  257.1 34.0 %reduce-scatter.5.cloned.1.call-start = ((), (), s32[]{:S(2)}) async-start(), calls=%async_computation.4 | async-start | bytes 1310720 | tf_op jit(solution)/shard_map/while/body/eval_jaxpr/reduce_scatter | solution.py:103
  259.1 0.7 copy-start.1
  266.1 1.0 copy-start
  293.0 15.9 %collective-permute-start.1 = (bf16[128,1024]{1,0:T(8,128)(2,1)S(1)}, bf16[128,1024]{1,0:T(8,128)(2,1)}, u32[]{:S(2)}, u32[]{:S(2)}) collective-permute-start(bf16[128,1024]{1,0:T(8,128)(2,1)S(1)} %get-tuple-element.834), channel_id=1, source_target_pairs={{16,0},{17,1},{18,2},{19,3},{20,4},{21,5},{22,6},{23,7},{24,8},{25... | collective-permute-start | bytes 786440 | tf_op jit(solution)/shard_map/while/body/eval_jaxpr/ppermute | solution.py:10
  308.9 153.2 %reduce-scatter.3.cloned.1.call-start = ((), (), s32[]{:S(2)}) async-start(), calls=%async_computation.2 | async-start | bytes 10485760 | tf_op jit(solution)/shard_map/reduce_scatter | solution.py:134
  318.1 35.9 %copy-start.4 = (f32[1,16]{1,0:T(1,128)S(1)}, f32[1,16]{1,0:T(1,128)}, u32[]{:S(2)}) copy-start(f32[1,16]{1,0:T(1,128)} %param.21) | copy-start | bytes 196
  318.1 37.1 %copy-start.2 = (f32[1,16]{1,0:T(1,128)S(1)}, f32[1,16]{1,0:T(1,128)}, u32[]{:S(2)}) copy-start(f32[1,16]{1,0:T(1,128)} %param.19) | copy-start | bytes 196
  318.1 37.1 %copy-start.3 = (f32[1,16]{1,0:T(1,128)S(1)}, f32[1,16]{1,0:T(1,128)}, u32[]{:S(2)}) copy-start(f32[1,16]{1,0:T(1,128)} %param.20) | copy-start | bytes 196
Sparse Core Ops, SparseCore 0:
  29.3 19.4 all-gather.1
  66.9 17.8 all-gather.1
  104.7 17.8 all-gather.1
  152.8 31.9 reduce-scatter.4
  206.6 32.6 reduce-scatter.4
  267.2 23.8 reduce-scatter.4
Sparse Core Ops, SparseCore 1:
  318.2 143.9 reduce-scatter.2
where the time goes:
time: 471 us; the launch traced here: 470 us
  waiting for transfers between devices  261 us (55%)
  other arithmetic  54.3 us (12%)
  matrix products  51.8 us (11%)
  blocking collectives  35.8 us (8%)
  local copies, waits for them, and re-layouts  25.2 us (5%)
  starting transfers between devices  19 us (4%)
  between operations  17.7 us (4%)
    reduce_scatter x1, waiting for transfers between devices, shards(): lax.psum_scatter(held.astype(jnp.bfloat16), 'dp', scatter_dimension=0, ti...  105 us
    reduce_scatter x3, waiting for transfers between devices, backward_tick(): lax.psum_scatter(partial_terms.astype(jnp.bfloat16), 'tensor', scatter_di...  86.1 us
    all_gather x3, waiting for transfers between devices, forward_tick(): quant_full = lax.all_gather(quant_local, 'tensor', axis=1, tiled=True)  49.4 us
    pmax x1, blocking collectives, shards(): lax.pmax((act_peak, weight_peak, grad_peak), ('dp', 'tensor'))  35.8 us
    dot_general x2, matrix products, backward_tick(): lax.dot_general(saved_acts, quant_grad, (((0,), (0,)), ((), ())), preferr...  27.7 us
    ppermute x6, waiting for transfers between devices, shifted(): lax.ppermute(value, axis, [(source, source + steps) for source in range(i...  20.5 us
    ppermute x6, starting transfers between devices, shifted(): lax.ppermute(value, axis, [(source, source + steps) for source in range(i...  18.9 us
    dynamic_update_slice x9, other arithmetic, place_row(): lax.dynamic_update_index_in_dim(buffer, jnp.where(is_live, new_row, old_r...  14.8 us
  transfers between devices with their start and end apart: 13, of which 11 were waited for; matrix products, arithmetic and copies ran while one was open for 9% of the time, Pallas kernels for 0%

commit v1 on v0

v1 whole, which is shorter than its diff:
```python
import functools

import jax
import jax.numpy as jnp
from jax import lax
from jax.experimental import pallas as pl
from jax.experimental.pallas import tpu as pltpu
from jax.sharding import PartitionSpec as P

MESH = pl.DeviceIdType.MESH
PIECES = 2
WIDE = 512


def strides_below(index, count):
    low = (index & -index) if index else count
    step, found = low // 2, []
    while step:
        found.append(step)
        step //= 2
    return found


def kernel(S, N, T, NC, RC, F, FA,
           acts, weights, cot, hist_a, hist_w, hist_g,
           out_acts, out_grads, out_w, out_ha, out_hw, out_hg,
           w, xin, xg, xout, acc, gin, part, rs, gout, G, A, dw, dwb, pk, amax, gmax,
           w_sem, x_ss, x_rs, ag_ss, ag_rs, g_ss, g_rs, rd_ss, rd_rs,
           G_ss, G_rs, A_ss, A_rs, B_ss, B_rs, p_ss, p_rs, o_sem, ow_sem):
    s, d, t = lax.axis_index("pipe"), lax.axis_index("dp"), lax.axis_index("tensor")
    last = S - 1
    bf, f32 = jnp.bfloat16, jnp.float32
    half = RC // 2

    def remote(src, dst, ss, rsem, **where):
        return pltpu.make_async_remote_copy(
            src_ref=src, dst_ref=dst, send_sem=ss, recv_sem=rsem,
            device_id=where, device_id_type=MESH)

    loads = [pltpu.make_async_copy(weights.at[b], w.at[b], w_sem.at[b]) for b in range(T)]
    for copy in loads:
        copy.start()

    barrier = pltpu.get_barrier_semaphore()
    for k in range(N):
        for j in range(T):
            if k or j:
                pl.semaphore_signal(barrier, inc=1, device_id={"dp": d ^ k, "tensor": t ^ j},
                                    device_id_type=MESH)

    @pl.when(s > 0)
    def _():
        pl.semaphore_signal(barrier, inc=1, device_id={"pipe": s - 1}, device_id_type=MESH)

    @pl.when(s < last)
    def _():
        pl.semaphore_signal(barrier, inc=1, device_id={"pipe": s + 1}, device_id_type=MESH)

    lim_a = jnp.max(hist_a[...], axis=1, keepdims=True).astype(bf)
    lim_w = jnp.max(hist_w[...], axis=1, keepdims=True).astype(bf)
    lim_g = jnp.max(hist_g[...], axis=1, keepdims=True).astype(bf)

    def clip(v, lim):
        return jnp.minimum(jnp.maximum(v, -lim), lim)

    def fold(v):
        return jnp.max(jnp.abs(v).reshape(-1, 16, v.shape[-1]), axis=0)

    amax[...] = jnp.zeros_like(amax)
    gmax[...] = jnp.zeros_like(gmax)

    near = (s > 0).astype(jnp.int32) + (s < last).astype(jnp.int32)
    pl.semaphore_wait(barrier, N * T - 1 + near)

    up = jnp.minimum(s + 1, last)
    down = jnp.maximum(s - 1, 0)

    def x_copy(c):
        return remote(xout.at[c], xin.at[c], x_ss.at[c], x_rs.at[c], pipe=up)

    def g_copy(c):
        return remote(gout.at[c], gin.at[c], g_ss.at[c], g_rs.at[c], pipe=down)

    def ag_copy(c, j, st):
        i = j ^ st
        return remote(xg.at[c, j], xg.at[c, i], ag_ss.at[c, i], ag_rs.at[c, i], tensor=t ^ st)

    def low(i):
        return i & -i

    def G_copy(c, j, st):
        i = j ^ st
        return remote(G.at[c, j], G.at[c, i], G_ss.at[c, i], G_rs.at[c, i], dp=d ^ st)

    ratio = N // T

    def in_block(r):
        start = lax.rem(r, ratio) * FA
        return t ^ lax.div(r, ratio), pl.ds(pl.multiple_of(start, FA), FA)

    def A_copy(c, k):
        rows = pl.ds(pl.multiple_of((t & 1) * half, half), half)
        owner, cols = in_block(d ^ k)
        return remote(xg.at[c, owner, rows, cols], A.at[c, k, rows], A_ss.at[c, k], A_rs.at[c, k],
                      dp=d ^ k)

    def B_copy(c, k):
        rows = pl.ds(pl.multiple_of((t & 1) * half, half), half)
        return remote(A.at[c, k, rows], A.at[c, k, rows], B_ss.at[c, k], B_rs.at[c, k],
                      tensor=t ^ 1)

    stages = []
    st = 1
    while st < T:
        stages.append(st)
        st *= 2

    def rd_copy(c, j, level):
        st = stages[level]
        i = j ^ st
        return remote(part.at[c, j], rs.at[c, level, i], rd_ss.at[c, j], rd_rs.at[c, level, i],
                      tensor=t ^ st)

    def prep(c):
        @pl.when(s == 0)
        def _():
            xin[c] = acts[c]

        @pl.when(s > 0)
        def _():
            x_copy(c).wait_recv()

        x = xin[c]
        xg[c, 0] = clip(x, lim_a)
        for st in strides_below(0, T):
            ag_copy(c, 0, st).start()
        amax[...] = jnp.maximum(amax[...], fold(x))

    def clip_weights():
        peak = jnp.zeros((16, F), bf)
        for b in range(T):
            loads[b].wait()

            def body(i, m, b=b):
                rows = pl.ds(pl.multiple_of(i * 128, 128), 128)
                v = w[b, rows]
                w[b, rows] = clip(v, lim_w)
                return jnp.maximum(m, fold(v))

            peak = lax.fori_loop(0, F // 128, body, peak)
        return jnp.max(peak.astype(f32), keepdims=True).reshape(1, 1)

    def compute(c):
        for j in range(T):
            if j:
                ag_copy(c, j ^ low(j), low(j)).wait_recv()
                for st in strides_below(j, T):
                    ag_copy(c, j, st).start()
            b = t ^ j

            def body(n, _, j=j, b=b):
                cols = pl.ds(pl.multiple_of(n * WIDE, WIDE), WIDE)
                y = jnp.dot(xg[c, j], w[b, :, cols], preferred_element_type=f32)
                if j == 0:
                    acc[:, cols] = y
                elif j < T - 1:
                    acc[:, cols] += y
                else:
                    xout[c, :, cols] = (acc[:, cols] + y + xin[c, :, cols].astype(f32)).astype(bf)
                return 0

            lax.fori_loop(0, F // WIDE, body, 0)

        @pl.when(s < last)
        def _():
            x_copy(c).start()

        pltpu.make_async_copy(xout.at[c], out_acts.at[c], o_sem.at[0, c]).start()
        for k in range(1, N):
            A_copy(c, k).start()
        owner, cols = in_block(d)
        A[c, 0] = xg[c, owner, :, cols]

    def prepb(c, is_last):
        if is_last:
            gin[c] = (cot[c].astype(f32) * xout[c].astype(f32)).astype(bf)
        else:
            g_copy(c).wait_recv()
        g = gin[c]
        G[c, 0] = clip(g, lim_g)
        for st in strides_below(0, N):
            G_copy(c, 0, st).start()
        gmax[...] = jnp.maximum(gmax[...], fold(g))
        order = sorted(range(T), key=lambda j: -(low(j) == 1))
        for j in order:
            b = t ^ j

            def body(n, _, j=j, b=b):
                cols = pl.ds(pl.multiple_of(n * WIDE, WIDE), WIDE)
                y = lax.dot_general(G[c, 0], w[b, cols, :], (((1,), (1,)), ((), ())),
                                    preferred_element_type=f32)
                part[c, j, :, cols] = y.astype(bf)
                return 0

            lax.fori_loop(0, F // WIDE, body, 0)
            if low(j) == 1:
                rd_copy(c, j, 0).start()

    def midb(c):
        for level in range(len(stages) - 1):
            st = stages[level]
            js = list(range(0, T, 2 * st))
            for j in sorted(js, key=lambda j: -(low(j) == 2 * st)):
                if j == 0:
                    continue
                rd_copy(c, j ^ st, level).wait_recv()
                part[c, j] = (part[c, j].astype(f32) + rs[c, level, j].astype(f32)).astype(bf)
                if low(j) == 2 * st:
                    rd_copy(c, j, level + 1).start()

    def finb(c):
        total = gin[c].astype(f32) + part[c, 0].astype(f32)
        for level in range(len(stages)):
            rd_copy(c, stages[level], level).wait_recv()
            total = total + rs[c, level, 0].astype(f32)
        gout[c] = total.astype(bf)

        @pl.when(s > 0)
        def _():
            g_copy(c).start()

        pltpu.make_async_copy(gout.at[c], out_grads.at[c], o_sem.at[1, c]).start()

    def relay_G(c):
        for j in range(1, N):
            G_copy(c, j ^ low(j), low(j)).wait_recv()
            for st in strides_below(j, N):
                G_copy(c, j, st).start()

    def relay_A(c):
        for k in range(1, N):
            A_copy(c, k).wait_recv()
            B_copy(c, k).start()

    def peers():
        return [(k, j) for k in range(N) for j in range(T) if k or j]

    def p_copy(k, j):
        i = k * T + j
        return remote(pk.at[0], pk.at[i], p_ss.at[i], p_rs.at[i], dp=d ^ k, tensor=t ^ j)

    def send_peaks():
        row = lax.broadcasted_iota(jnp.int32, (8, 128), 0)
        top_a = jnp.max(amax[...].astype(f32), keepdims=True).reshape(1, 1)
        top_g = jnp.max(gmax[...].astype(f32), keepdims=True).reshape(1, 1)
        pk[0] = jnp.where(row == 0, top_a, jnp.where(row == 1, w_peak, top_g))
        for k, j in peers():
            p_copy(k, j).start()

    prep(0)
    if NC > 1:
        prep(1)
    w_peak = clip_weights()

    def backward(i, is_last):
        if i < NC:
            prepb(i, is_last)
            if i == NC - 1:
                send_peaks()
            midb(i)
        if 1 <= i <= NC:
            finb(i - 1)

    @pl.when(s == last)
    def _():
        for c in range(NC):
            compute(c)
            if c + 2 < NC:
                prep(c + 2)
            if c >= 1:
                backward(c - 1, True)
        backward(NC - 1, True)
        backward(NC, True)
        for c in range(NC):
            relay_A(c)
            relay_G(c)

    @pl.when(s < last)
    def _():
        for c in range(NC):
            compute(c)
            if c + 2 < NC:
                prep(c + 2)
        for c in range(NC):
            relay_A(c)
        for c in range(NC + 1):
            backward(c, False)
            if c >= 1:
                relay_G(c - 1)

    for c in range(NC):
        for k in range(1, N):
            B_copy(c, k).wait_recv()
        tile = 256

        def body(n, _, c=c):
            cols = pl.ds(pl.multiple_of(n * tile, tile), tile)
            y = lax.dot_general(A[c, :, :, cols].reshape(N * RC, tile), G[c].reshape(N * RC, F),
                                (((0,), (0,)), ((), ())), preferred_element_type=f32)
            if c == 0:
                dw[cols, :] = y
            elif c < NC - 1:
                dw[cols, :] += y
            else:
                dwb[cols, :] = (dw[cols, :] + y).astype(bf)
            return 0

        lax.fori_loop(0, FA // tile, body, 0)
    out = pltpu.make_async_copy(dwb, out_w, ow_sem)
    out.start()

    for k, j in peers():
        p_copy(k, j).wait_recv()
    top = jnp.max(pk[...], axis=0)
    for row, (hist, out_hist) in enumerate(((hist_a, out_ha), (hist_w, out_hw), (hist_g, out_hg))):
        old = hist[...]
        out_hist[...] = jnp.concatenate([top[row:row + 1, 0:1], old[:, :-1]], axis=1)

    for c in range(NC):
        for i in range(1, T):
            ag_copy(c, i ^ low(i), low(i)).wait_send()
        for level, st in enumerate(stages):
            for j in range(0, T, st):
                if j & st:
                    rd_copy(c, j, level).wait_send()
        for i in range(1, N):
            G_copy(c, i ^ low(i), low(i)).wait_send()
            A_copy(c, i).wait_send()
            B_copy(c, i).wait_send()
        pltpu.make_async_copy(xout.at[c], out_acts.at[c], o_sem.at[0, c]).wait()
        pltpu.make_async_copy(gout.at[c], out_grads.at[c], o_sem.at[1, c]).wait()

        @pl.when(s < last)
        def _():
            x_copy(c).wait_send()

        @pl.when(s > 0)
        def _():
            g_copy(c).wait_send()

    for k, j in peers():
        p_copy(k, j).wait_send()
    out.wait()


def shards(acts_in, weights, cotangent, hist_act, hist_weight, hist_grad):
    S, N, T = lax.axis_size("pipe"), lax.axis_size("dp"), lax.axis_size("tensor")
    M, R, F = acts_in.shape
    NC, RC = M * PIECES, R // PIECES
    FA = T * F // N
    bf, f32 = jnp.bfloat16, jnp.float32
    levels = max(1, T.bit_length() - 1)
    dma = pltpu.SemaphoreType.DMA
    vmem = pl.BlockSpec(memory_space=pltpu.VMEM)
    anyw = pl.BlockSpec(memory_space=pl.ANY)
    hist = jax.ShapeDtypeStruct(hist_act.shape, f32)
    chunk = (NC, RC, F)
    result = pl.pallas_call(
        functools.partial(kernel, S, N, T, NC, RC, F, FA),
        out_shape=(jax.ShapeDtypeStruct(chunk, bf), jax.ShapeDtypeStruct(chunk, bf),
                   jax.ShapeDtypeStruct((FA, F), bf), hist, hist, hist),
        in_specs=[vmem, anyw, vmem, vmem, vmem, vmem],
        out_specs=(anyw, anyw, anyw, vmem, vmem, vmem),
        scratch_shapes=[
            pltpu.VMEM((T, F, F), bf),
            pltpu.VMEM(chunk, bf),
            pltpu.VMEM((NC, T, RC, F), bf),
            pltpu.VMEM(chunk, bf),
            pltpu.VMEM((RC, F), f32),
            pltpu.VMEM(chunk, bf),
            pltpu.VMEM((NC, T, RC, F), bf),
            pltpu.VMEM((NC, levels, T, RC, F), bf),
            pltpu.VMEM(chunk, bf),
            pltpu.VMEM((NC, N, RC, F), bf),
            pltpu.VMEM((NC, N, RC, FA), bf),
            pltpu.VMEM((FA, F), f32),
            pltpu.VMEM((FA, F), bf),
            pltpu.VMEM((N * T, 8, 128), f32),
            pltpu.VMEM((16, F), bf),
            pltpu.VMEM((16, F), bf),
            dma((T,)), dma((NC,)), dma((NC,)), dma((NC, T)), dma((NC, T)),
            dma((NC,)), dma((NC,)), dma((NC, T)), dma((NC, levels, T)),
            dma((NC, N)), dma((NC, N)), dma((NC, N)), dma((NC, N)), dma((NC, N)), dma((NC, N)),
            dma((N * T,)), dma((N * T,)), dma((2, NC)), dma(()),
        ],
        compiler_params=pltpu.CompilerParams(
            collective_id=0, has_side_effects=True, vmem_limit_bytes=60 * 2**20),
    )(acts_in.reshape(chunk), weights.reshape(T, F, F), cotangent.reshape(chunk),
      hist_act, hist_weight, hist_grad)
    out_acts, out_grads, out_w, ha, hw, hg = result
    return (out_acts.reshape(1, M, R, F), out_grads.reshape(1, M, R, F), out_w[None], ha, hw, hg)


def solution(mesh):
    placed = (P(None, "dp", "tensor"), P("pipe", None, "tensor"), P(None, "dp", "tensor"),
              P("pipe", None), P("pipe", None), P("pipe", None))
    return jax.shard_map(
        shards, mesh=mesh, in_specs=placed,
        out_specs=(P("pipe", None, "dp", "tensor"), P("pipe", None, "dp", "tensor"),
                   P("pipe", "dp", "tensor"), P("pipe", None), P("pipe", None), P("pipe", None)),
        check_vma=False)
```

time: 471 us -> 101 us (0.21)
  waiting for transfers between devices: 261 us -> 0 us
  Pallas kernels: 0 us -> 93.7 us
  other arithmetic: 54.3 us -> 0 us
  matrix products: 51.8 us -> 0 us
  blocking collectives: 35.8 us -> 0 us
  starting transfers between devices: 19 us -> 0 us
  local copies, waits for them, and re-layouts: 25.2 us -> 6.75 us
  between operations: 17.7 us -> 0.66 us
    reduce_scatter x4 -> x0, waiting for transfers between devices: 191 us -> none  [the longest x1 105 us: shards(): lax.psum_scatter(held.astype(jnp.bfloat16), 'dp', scatter_dimension=0, ti...]
    pallas_call x0 -> x1, Pallas kernels: none -> 93.7 us  [shards(): pl.pallas_call(functools.partial(kernel, S, N, T, NC, RC, F, FA), out_sha...]
    dot_general x6 -> x0, matrix products: 51.8 us -> none  [the longest x2 27.7 us: backward_tick(): lax.dot_general(saved_acts, quant_grad, (((0,), (0,)), ((), ())), preferr...]
    all_gather x3 -> x0, waiting for transfers between devices: 49.4 us -> none  [forward_tick(): quant_full = lax.all_gather(quant_local, 'tensor', axis=1, tiled=True)]
    pmax x1 -> x0, blocking collectives: 35.8 us -> none  [shards(): lax.pmax((act_peak, weight_peak, grad_peak), ('dp', 'tensor'))]
    reduce_max x10 -> x0, other arithmetic: 24.9 us -> none  [the longest x1 10.5 us: shards(): weight_peak = jnp.max(jnp.abs(weight.astype(jnp.float32)))]
    ppermute x6 -> x0, waiting for transfers between devices: 20.5 us -> none  [shifted(): lax.ppermute(value, axis, [(source, source + steps) for source in range(i...]
    ppermute x6 -> x0, starting transfers between devices: 18.9 us -> none  [shifted(): lax.ppermute(value, axis, [(source, source + steps) for source in range(i...]
  transfers between devices with their start and end apart: 13 -> 0, of which waited for: 11 -> 0; matrix products, arithmetic and copies ran while one was open for 9% -> 0% of each run, Pallas kernels for 0% -> 0%
where the time goes in v1:
time: 101 us
  Pallas kernels  93.7 us (93%)
  local copies, waits for them, and re-layouts  6.75 us (7%)
    pallas_call x1, Pallas kernels, shards(): pl.pallas_call(functools.partial(kernel, S, N, T, NC, RC, F, FA), out_sha...  93.7 us
    unnamed x14, local copies, waits for them, and re-layouts  6.75 us

profile of v1, /device:TPU:0, one launch (start us, length us, event | category | flops | bytes accessed | tf_op | source)
XLA Modules:
  0.0 101.1 jit_solution(12715537475645264960)
XLA Ops:
  0.6 93.7 %shard_map.109 = (bf16[4,64,1024]{2,1,0:T(8,128)(2,1)}, bf16[4,64,1024]{2,1,0:T(8,128)(2,1)}, bf16[1024,1024]{1,0:T(8,128)(2,1)}, f32[1,16]{1,0:T(1,128)}, f32[1,16]{1,0:T(1,128)}, /*index=5*/f32[1,16]{1,0:T(1,128)}) custom-call(bf16[4,64,1024]{2,1,0:T(8,128)(2,1)} %bitcast.8, bf16[4,1024,1024]{2,1,0:T(8,128)(2,1)} %bitcast.6, bf16[4,64,1024]{2,1,0:T(8,128)(2,1)} %bitcast.9, ...), custom_call_target="tpu_custom_call" | custom-call | tf_op jit(solution)/shard_map/pallas_call | solution.py:368
  94.3 0.0 copy-start
  94.3 2.0 %copy.18 = bf16[1,2,128,1024]{3,2,1,0:T(8,128)(2,1)} copy(bf16[1,2,128,1024]{3,2,1,0:T(8,128)(2,1)} %bitcast.11) | data formatting | bytes 1048576
  96.3 1.9 %copy.19 = bf16[1,2,128,1024]{3,2,1,0:T(8,128)(2,1)} copy(bf16[1,2,128,1024]{3,2,1,0:T(8,128)(2,1)} %bitcast.10) | data formatting | bytes 1048576
  98.2 0.0 copy-done
  98.2 0.0 copy-start.3
  98.2 0.0 copy-start.2
  98.2 0.0 copy-start.1
  98.2 1.3 %copy.20 = bf16[1,1024,1024]{2,1,0:T(8,128)(2,1)} copy(bf16[1,1024,1024]{2,1,0:T(8,128)(2,1)S(1)} %bitcast.7) | data formatting | bytes 4194304
  99.6 0.0 copy-done.3
  99.6 0.5 copy.21
  100.1 0.0 copy-done.2
  100.1 0.5 copy.22
  100.6 0.0 copy-done.1
  100.6 0.5 copy.23
Async XLA Ops:
  94.3 3.9 %copy-start = (bf16[1024,1024]{1,0:T(8,128)(2,1)S(1)}, bf16[1024,1024]{1,0:T(8,128)(2,1)}, u32[]{:S(2)}) copy-start(bf16[1024,1024]{1,0:T(8,128)(2,1)} %get-tuple-element.14) | copy-start | bytes 6291460
  98.2 1.3 %copy-start.3 = (f32[1,16]{1,0:T(1,128)S(1)}, f32[1,16]{1,0:T(1,128)}, u32[]{:S(2)}) copy-start(f32[1,16]{1,0:T(1,128)} %get-tuple-element.27) | copy-start | bytes 196
  98.2 1.8 %copy-start.2 = (f32[1,16]{1,0:T(1,128)S(1)}, f32[1,16]{1,0:T(1,128)}, u32[]{:S(2)}) copy-start(f32[1,16]{1,0:T(1,128)} %get-tuple-element.28) | copy-start | bytes 196
  98.2 2.4 %copy-start.1 = (f32[1,16]{1,0:T(1,128)S(1)}, f32[1,16]{1,0:T(1,128)}, u32[]{:S(2)}) copy-start(f32[1,16]{1,0:T(1,128)} %get-tuple-element.29) | copy-start | bytes 196

commit v2 on v1

--- a/solution.py
+++ b/solution.py
@@ -30,7 +30,6 @@
     s, d, t = lax.axis_index("pipe"), lax.axis_index("dp"), lax.axis_index("tensor")
     last = S - 1
     bf, f32 = jnp.bfloat16, jnp.float32
-    half = RC // 2
 
     def remote(src, dst, ss, rsem, **where):
         return pltpu.make_async_remote_copy(
@@ -98,16 +97,24 @@
         start = lax.rem(r, ratio) * FA
         return t ^ lax.div(r, ratio), pl.ds(pl.multiple_of(start, FA), FA)
 
+    piece = RC // T
+
+    def rows_of(owner):
+        return pl.ds(pl.multiple_of(owner * piece, piece), piece)
+
     def A_copy(c, k):
-        rows = pl.ds(pl.multiple_of((t & 1) * half, half), half)
         owner, cols = in_block(d ^ k)
-        return remote(xg.at[c, owner, rows, cols], A.at[c, k, rows], A_ss.at[c, k], A_rs.at[c, k],
-                      dp=d ^ k)
-
-    def B_copy(c, k):
-        rows = pl.ds(pl.multiple_of((t & 1) * half, half), half)
-        return remote(A.at[c, k, rows], A.at[c, k, rows], B_ss.at[c, k], B_rs.at[c, k],
-                      tensor=t ^ 1)
+        return remote(xg.at[c, owner, rows_of(t), cols], A.at[c, k, rows_of(t)],
+                      A_ss.at[c, k], A_rs.at[c, k], dp=d ^ k)
+
+    def B_copy(c, j, st):
+        i = j ^ st
+        there = A.at[c, pl.ds(1, N - 1), rows_of(t ^ j)]
+        return remote(there, there, B_ss.at[c, i], B_rs.at[c, i], tensor=t ^ st)
+
+    def B_arrival(c, i):
+        there = A.at[c, pl.ds(1, N - 1), rows_of(t ^ i)]
+        return remote(there, there, B_ss.at[c, i], B_rs.at[c, i], tensor=t ^ low(i))
 
     stages = []
     st = 1
@@ -233,77 +240,34 @@
 
     def relay_G(c):
         for j in range(1, N):
-            G_copy(c, j ^ low(j), low(j)).wait_recv()
-            for st in strides_below(j, N):
-                G_copy(c, j, st).start()
+            if strides_below(j, N):
+                G_copy(c, j ^ low(j), low(j)).wait_recv()
+                for st in strides_below(j, N):
+                    G_copy(c, j, st).start()
 
     def relay_A(c):
         for k in range(1, N):
             A_copy(c, k).wait_recv()
-            B_copy(c, k).start()
-
-    def peers():
-        return [(k, j) for k in range(N) for j in range(T) if k or j]
-
-    def p_copy(k, j):
-        i = k * T + j
-        return remote(pk.at[0], pk.at[i], p_ss.at[i], p_rs.at[i], dp=d ^ k, tensor=t ^ j)
-
-    def send_peaks():
-        row = lax.broadcasted_iota(jnp.int32, (8, 128), 0)
-        top_a = jnp.max(amax[...].astype(f32), keepdims=True).reshape(1, 1)
-        top_g = jnp.max(gmax[...].astype(f32), keepdims=True).reshape(1, 1)
-        pk[0] = jnp.where(row == 0, top_a, jnp.where(row == 1, w_peak, top_g))
-        for k, j in peers():
-            p_copy(k, j).start()
-
-    prep(0)
-    if NC > 1:
-        prep(1)
-    w_peak = clip_weights()
-
-    def backward(i, is_last):
-        if i < NC:
-            prepb(i, is_last)
-            if i == NC - 1:
-                send_peaks()
-            midb(i)
-        if 1 <= i <= NC:
-            finb(i - 1)
-
-    @pl.when(s == last)
-    def _():
-        for c in range(NC):
-            compute(c)
-            if c + 2 < NC:
-                prep(c + 2)
-            if c >= 1:
-                backward(c - 1, True)
-        backward(NC - 1, True)
-        backward(NC, True)
-        for c in range(NC):
-            relay_A(c)
-            relay_G(c)
-
-    @pl.when(s < last)
-    def _():
-        for c in range(NC):
-            compute(c)
-            if c + 2 < NC:
-                prep(c + 2)
-        for c in range(NC):
-            relay_A(c)
-        for c in range(NC + 1):
-            backward(c, False)
-            if c >= 1:
-                relay_G(c - 1)
-
-    for c in range(NC):
-        for k in range(1, N):
-            B_copy(c, k).wait_recv()
+        for st in strides_below(0, T):
+            B_copy(c, 0, st).start()
+
+    def relay_B(c):
+        for j in range(1, T):
+            if strides_below(j, T):
+                B_arrival(c, j).wait_recv()
+                for st in strides_below(j, T):
+                    B_copy(c, j, st).start()
+
+    def update(c):
+        for j in range(1, N):
+            if not strides_below(j, N):
+                G_copy(c, j ^ low(j), low(j)).wait_recv()
+        for j in range(1, T):
+            if not strides_below(j, T):
+                B_arrival(c, j).wait_recv()
         tile = 256
 
-        def body(n, _, c=c):
+        def body(n, _):
             cols = pl.ds(pl.multiple_of(n * tile, tile), tile)
             y = lax.dot_general(A[c, :, :, cols].reshape(N * RC, tile), G[c].reshape(N * RC, F),
                                 (((0,), (0,)), ((), ())), preferred_element_type=f32)
@@ -316,6 +280,74 @@
             return 0
 
         lax.fori_loop(0, FA // tile, body, 0)
+
+    def peers():
+        return [(k, j) for k in range(N) for j in range(T) if k or j]
+
+    def p_copy(k, j):
+        i = k * T + j
+        return remote(pk.at[0], pk.at[i], p_ss.at[i], p_rs.at[i], dp=d ^ k, tensor=t ^ j)
+
+    def send_peaks():
+        row = lax.broadcasted_iota(jnp.int32, (8, 128), 0)
+        top_a = jnp.max(amax[...].astype(f32), keepdims=True).reshape(1, 1)
+        top_g = jnp.max(gmax[...].astype(f32), keepdims=True).reshape(1, 1)
+        pk[0] = jnp.where(row == 0, top_a, jnp.where(row == 1, w_peak, top_g))
+        for k, j in peers():
+            p_copy(k, j).start()
+
+    prep(0)
+    if NC > 1:
+        prep(1)
+    w_peak = clip_weights()
+
+    def backward(i, is_last):
+        if i < NC:
+            prepb(i, is_last)
+            if i == NC - 1:
+                send_peaks()
+            midb(i)
+        if 1 <= i <= NC:
+            finb(i - 1)
+
+    @pl.when(s == last)
+    def _():
+        for c in range(NC):
+            compute(c)
+            if c + 2 < NC:
+                prep(c + 2)
+            if c >= 1:
+                backward(c - 1, True)
+        backward(NC - 1, True)
+        backward(NC, True)
+        for c in range(NC):
+            relay_A(c)
+            relay_G(c)
+        for c in range(NC):
+            relay_B(c)
+        for c in range(NC - 1):
+            update(c)
+
+    @pl.when(s < last)
+    def _():
+        for c in range(NC):
+            compute(c)
+            if c + 2 < NC:
+                prep(c + 2)
+        for c in range(NC):
+            relay_A(c)
+        for c in range(NC):
+            relay_B(c)
+        for c in range(NC + 1):
+            backward(c, False)
+            if c >= 1:
+                relay_G(c - 1)
+            if c >= 3:
+                update(c - 3)
+        for c in range(NC - 2, NC - 1):
+            update(c)
+
+    update(NC - 1)
     out = pltpu.make_async_copy(dwb, out_w, ow_sem)
     out.start()
 
@@ -336,7 +368,8 @@
         for i in range(1, N):
             G_copy(c, i ^ low(i), low(i)).wait_send()
             A_copy(c, i).wait_send()
-            B_copy(c, i).wait_send()
+        for i in range(1, T):
+            B_copy(c, i ^ low(i), low(i)).wait_send()
         pltpu.make_async_copy(xout.at[c], out_acts.at[c], o_sem.at[0, c]).wait()
         pltpu.make_async_copy(gout.at[c], out_grads.at[c], o_sem.at[1, c]).wait()
 
@@ -390,7 +423,7 @@
             pltpu.VMEM((16, F), bf),
             dma((T,)), dma((NC,)), dma((NC,)), dma((NC, T)), dma((NC, T)),
             dma((NC,)), dma((NC,)), dma((NC, T)), dma((NC, levels, T)),
-            dma((NC, N)), dma((NC, N)), dma((NC, N)), dma((NC, N)), dma((NC, N)), dma((NC, N)),
+            dma((NC, N)), dma((NC, N)), dma((NC, N)), dma((NC, N)), dma((NC, T)), dma((NC, T)),
             dma((N * T,)), dma((N * T,)), dma((2, NC)), dma(()),
         ],
         compiler_params=pltpu.CompilerParams(

time: 101 us -> 93.9 us (0.930)
  Pallas kernels: 93.7 us -> 86.3 us
    pallas_call x1, Pallas kernels: 93.7 us -> 86.3 us  [shards(): pl.pallas_call(functools.partial(kernel, S, N, T, NC, RC, F, FA), out_sha...]
where the time goes in v2:
time: 93.9 us; the launch traced here: 93.7 us
  Pallas kernels  86.3 us (92%)
  local copies, waits for them, and re-layouts  6.75 us (7%)
    pallas_call x1, Pallas kernels, shards(): pl.pallas_call(functools.partial(kernel, S, N, T, NC, RC, F, FA), out_sha...  86.3 us
    unnamed x14, local copies, waits for them, and re-layouts  6.75 us

profile of v2, /device:TPU:0, one launch (start us, length us, event | category | flops | bytes accessed | tf_op | source)
XLA Modules:
  0.0 93.7 jit_solution(14246399733620298568)
XLA Ops:
  0.6 86.3 %shard_map.109 = (bf16[4,64,1024]{2,1,0:T(8,128)(2,1)}, bf16[4,64,1024]{2,1,0:T(8,128)(2,1)}, bf16[1024,1024]{1,0:T(8,128)(2,1)}, f32[1,16]{1,0:T(1,128)}, f32[1,16]{1,0:T(1,128)}, /*index=5*/f32[1,16]{1,0:T(1,128)}) custom-call(bf16[4,64,1024]{2,1,0:T(8,128)(2,1)} %bitcast.8, bf16[4,1024,1024]{2,1,0:T(8,128)(2,1)} %bitcast.6, bf16[4,64,1024]{2,1,0:T(8,128)(2,1)} %bitcast.9, ...), custom_call_target="tpu_custom_call" | custom-call | tf_op jit(solution)/shard_map/pallas_call | solution.py:401
  86.9 0.0 copy-start
  87.0 2.0 %copy.18 = bf16[1,2,128,1024]{3,2,1,0:T(8,128)(2,1)} copy(bf16[1,2,128,1024]{3,2,1,0:T(8,128)(2,1)} %bitcast.11) | data formatting | bytes 1048576
  89.0 1.9 %copy.19 = bf16[1,2,128,1024]{3,2,1,0:T(8,128)(2,1)} copy(bf16[1,2,128,1024]{3,2,1,0:T(8,128)(2,1)} %bitcast.10) | data formatting | bytes 1048576
  90.8 0.0 copy-done
  90.8 0.0 copy-start.3
  90.8 0.0 copy-start.2
  90.8 0.0 copy-start.1
  90.9 1.3 %copy.20 = bf16[1,1024,1024]{2,1,0:T(8,128)(2,1)} copy(bf16[1,1024,1024]{2,1,0:T(8,128)(2,1)S(1)} %bitcast.7) | data formatting | bytes 4194304
  92.2 0.0 copy-done.3
  92.2 0.5 copy.21
  92.7 0.0 copy-done.2
  92.7 0.5 copy.22
  93.2 0.0 copy-done.1
  93.2 0.5 copy.23
Async XLA Ops:
  86.9 3.9 %copy-start = (bf16[1024,1024]{1,0:T(8,128)(2,1)S(1)}, bf16[1024,1024]{1,0:T(8,128)(2,1)}, u32[]{:S(2)}) copy-start(bf16[1024,1024]{1,0:T(8,128)(2,1)} %get-tuple-element.14) | copy-start | bytes 6291460
  90.8 1.3 %copy-start.3 = (f32[1,16]{1,0:T(1,128)S(1)}, f32[1,16]{1,0:T(1,128)}, u32[]{:S(2)}) copy-start(f32[1,16]{1,0:T(1,128)} %get-tuple-element.27) | copy-start | bytes 196
  90.8 1.8 %copy-start.2 = (f32[1,16]{1,0:T(1,128)S(1)}, f32[1,16]{1,0:T(1,128)}, u32[]{:S(2)}) copy-start(f32[1,16]{1,0:T(1,128)} %get-tuple-element.28) | copy-start | bytes 196
  90.8 2.4 %copy-start.1 = (f32[1,16]{1,0:T(1,128)S(1)}, f32[1,16]{1,0:T(1,128)}, u32[]{:S(2)}) copy-start(f32[1,16]{1,0:T(1,128)} %get-tuple-element.29) | copy-start | bytes 196
